TPU v7x, 32 devices: a whole 2x2x4 slice. The times are simulated.
32 devices in a mesh: section: 2 (over y), dp: 4 (over x, core), mp: 4 (over z).
Axes of the slice: x: 2, y: 2, z: 4, core: 2. Of those that a mesh axis runs over, the one named last changes fastest.
Arguments:
- patches: bfloat16 [4096, 1280], P(('section', 'dp')), may hold values from -6 to 6
- patch_counts: int32 [16], P(('section', 'dp')), may hold values from 64 to 256, as said below
- dest_rows: int32 [1024], P(('section', 'dp')), may hold values from 0 to 4095, as said below
- qkv_weight: bfloat16 [1280, 3, 1280], P(None, None, 'mp'), may hold values from -1 to 1
- out_weight: bfloat16 [1280, 1280], P('mp'), may hold values from -0.15625 to 0.15625
- attn_gain: bfloat16 [1280], replicated, may hold values from 0.25 to 1.75
- merge_gain: bfloat16 [1280], replicated, may hold values from 0.25 to 1.75
- fc1_weight: bfloat16 [5120, 5120], P('mp', ('section', 'dp')), may hold values from -0.078125 to 0.078125
- fc1_bias: bfloat16 [5120], P(('section', 'dp')), may hold values from -3 to 3
- fc2_weight: bfloat16 [5120, 8192], P(('section', 'dp'), 'mp'), may hold values from -0.078125 to 0.078125
- fc2_bias: bfloat16 [8192], P('mp'), may hold values from -3 to 3
- text_embeds: bfloat16 [4096, 8192], P(('section', 'dp'), 'mp'), may hold values from -6 to 6
- section_hidden: bfloat16 [4096, 8192], P(('section', 'dp'), 'mp'), may hold values from -80 to 80
- llm_gain: bfloat16 [8192], P('mp'), may hold values from 0.25 to 1.75
Outputs:
- sequence_embeds: bfloat16 [4096, 8192], P(('section', 'dp'), 'mp')
- layer_inputs: bfloat16 [4096, 8192], P(('section', 'dp'), 'mp')
Inputs may be any that keep to these rules, and one draw needn't show every extreme that they name: `patch_counts`: multiples of 4; a tile's patches fill the first slots of its block. `dest_rows`: all rows differ. Each group's merged slots form runs of 16 consecutive slots (aligned); a run goes to one sequence slice (row // 512, numbered in section-major order), different runs of a group to different slices. Rows of slots that are not live are never written.
All inputs are finite; a program needn't handle non-finite values.
Results may differ from a plain program's by a relative error of at most 0.0055.
Values may be sent and summed in bfloat16 or wider, within the bound.
No kernel may reach another device: no remote copies, remote signals or barrier semaphores. Data moves between devices by JAX's collectives and lax.ppermute only.
A program may use at most 128 MiB of HBM per device.

v0:
```python
import jax
import jax.numpy as jnp
from jax import lax
from jax.sharding import PartitionSpec as P

HEAD_DIM = 80
HID = 8192


vit_eps = 1e-06
llm_eps = 1e-06


def from_behind(value, axis, steps):
    count = lax.axis_size(axis)
    first, last = (max(0, -steps), min(count, count - steps))
    return lax.ppermute(value, axis, [(source, source + steps) for source in range(first, last)])


def layer_norm(values, gain):
    centred = values.astype(jnp.float32)
    centred = centred - jnp.mean(centred, axis=-1, keepdims=True)
    variance = jnp.mean(centred * centred, axis=-1, keepdims=True)
    return centred * lax.rsqrt(variance + vit_eps) * gain.astype(jnp.float32)


def per_device(
    patches,
    patch_counts,
    dest_rows,
    qkv_weight,
    out_weight,
    attn_gain,
    merge_gain,
    fc1_weight,
    fc1_bias,
    fc2_weight,
    fc2_bias,
    text_embeds,
    section_hidden,
    llm_gain,
):
    width = patches.shape[1]
    tile_total = patch_counts.shape[0]
    block_rows = patches.shape[0] // tile_total
    merged_rows = patches.shape[0] // 4
    local_cols = qkv_weight.shape[2]
    local_heads = local_cols // HEAD_DIM
    feature_cols = text_embeds.shape[1]
    seq_rows = text_embeds.shape[0]
    section_count = lax.axis_size("section")
    group_count = section_count * lax.axis_size("dp")
    run_cap = max(2, merged_rows // group_count)
    run_total = merged_rows // run_cap
    normed_in = layer_norm(patches, attn_gain).astype(jnp.bfloat16)
    projections = jnp.dot(
        normed_in, qkv_weight.reshape(width, 3 * local_cols), preferred_element_type=jnp.float32
    ).astype(jnp.bfloat16)
    projections = projections.reshape(tile_total, block_rows, 3, local_heads, HEAD_DIM)
    query_part = projections[:, :, 0]
    key_part = projections[:, :, 1]
    value_part = projections[:, :, 2]
    scores = jnp.einsum(
        "tqhd,tkhd->thqk", query_part, key_part, preferred_element_type=jnp.float32
    ) * HEAD_DIM ** (-0.5)
    key_live = (
        jnp.arange(block_rows, dtype=jnp.int32)[None, None, None, :]
        < patch_counts[:, None, None, None]
    )
    scores = jnp.where(key_live, scores, -1e30)
    weights = jax.nn.softmax(scores, axis=-1).astype(jnp.bfloat16)
    attended = jnp.einsum(
        "thqk,tkhd->tqhd", weights, value_part, preferred_element_type=jnp.float32
    ).astype(jnp.bfloat16)
    attended = attended.reshape(patches.shape[0], local_cols)
    partial_proj = jnp.dot(attended, out_weight, preferred_element_type=jnp.float32)
    position = lax.axis_index("mp")
    own_patch = lax.dynamic_slice_in_dim(
        patches.reshape(merged_rows, 4, width), position, 1, 1
    ).reshape(merged_rows, width)
    own_proj = lax.psum_scatter(
        partial_proj.reshape(merged_rows, 4, width), "mp", scatter_dimension=1, tiled=True
    ).reshape(merged_rows, width)
    block_out = (own_patch.astype(jnp.float32) + own_proj).astype(jnp.bfloat16)
    merge_part = layer_norm(block_out, merge_gain).astype(jnp.bfloat16)
    first_full, second_full, bias_full = (
        lax.all_gather(fc1_weight, "section", axis=1, tiled=True),
        lax.all_gather(fc2_weight, "section", axis=0, tiled=True),
        lax.all_gather(fc1_bias, "section", axis=0, tiled=True),
    )
    first_partial = jnp.dot(
        lax.all_gather(merge_part, "dp", axis=0, tiled=True),
        first_full,
        preferred_element_type=jnp.float32,
    )
    first_total = lax.psum(first_partial, "mp")
    hidden = jax.nn.gelu(first_total + bias_full.astype(jnp.float32), approximate=False).astype(
        jnp.bfloat16
    )
    embed_total = lax.psum_scatter(
        jnp.dot(hidden, second_full, preferred_element_type=jnp.float32).astype(jnp.bfloat16),
        "dp",
        scatter_dimension=0,
        tiled=True,
    ).astype(jnp.float32)
    image_embeds = (embed_total + fc2_bias.astype(jnp.float32)).astype(jnp.bfloat16)
    slot_in_tile = jnp.arange(merged_rows, dtype=jnp.int32) % (block_rows // 4)
    tile_counts = jnp.repeat(patch_counts, block_rows // 4, total_repeat_length=merged_rows)
    live = slot_in_tile * 4 < tile_counts
    receiver = dest_rows // seq_rows
    run_target = receiver.reshape(run_total, run_cap)[:, 0]
    place = jnp.where(live, dest_rows % seq_rows, seq_rows)
    send_rows = (
        jnp.zeros((group_count, run_cap, feature_cols), jnp.bfloat16)
        .at[run_target]
        .set(image_embeds.reshape(run_total, run_cap, feature_cols))
    )
    send_place = (
        jnp.full((group_count, run_cap), seq_rows, jnp.int32)
        .at[run_target]
        .set(place.reshape(run_total, run_cap))
    )
    got_rows, got_place = (
        lax.all_to_all(send_rows, ("section", "dp"), split_axis=0, concat_axis=0, tiled=True),
        lax.all_to_all(send_place, ("section", "dp"), split_axis=0, concat_axis=0, tiled=True),
    )
    sequence_embeds = text_embeds.at[got_place.reshape(-1)].set(
        got_rows.reshape(-1, feature_cols), mode="drop"
    )
    incoming = from_behind(section_hidden, "section", 1)
    entering = jnp.where(lax.axis_index("section") == 0, sequence_embeds, incoming).astype(
        jnp.float32
    )
    row_total = lax.psum(jnp.sum(entering * entering, axis=1), "mp")
    layer_inputs = (
        entering * lax.rsqrt(row_total / HID + llm_eps)[:, None] * llm_gain.astype(jnp.float32)
    ).astype(jnp.bfloat16)
    return (sequence_embeds, layer_inputs)


def solution(mesh):
    in_specs = (
        P(("section", "dp"), None),
        P(("section", "dp")),
        P(("section", "dp")),
        P(None, None, "mp"),
        P("mp", None),
        P(),
        P(),
        P("mp", ("section", "dp")),
        P(("section", "dp")),
        P(("section", "dp"), "mp"),
        P("mp"),
        P(("section", "dp"), "mp"),
        P(("section", "dp"), "mp"),
        P("mp"),
    )
    out_specs = (P(("section", "dp"), "mp"), P(("section", "dp"), "mp"))
    return jax.shard_map(
        per_device, mesh=mesh, in_specs=in_specs, out_specs=out_specs, check_vma=False
    )
```

profile of v0, /device:TPU:0, one launch (start us, length us, event | category | flops | bytes accessed | tf_op | source)
XLA Modules:
  0.0 317.5 jit_solution(10290408837068384715)
XLA Ops:
  8.1 3.3 %copy.70 = bf16[512,2048]{1,0:T(8,128)(2,1)} copy(bf16[512,2048]{1,0:T(8,128)(2,1)} %param.27) | data formatting | bytes 4194304
  11.4 0.2 convert_reduce_fusion
  11.7 0.5 fusion.6
  12.2 2.6 convolution_convert_fusion.1
  14.8 2.5 reshape.162
  17.3 1.6 fusion.107
  18.9 3.3 %fusion.109 = (f32[2,4,256]{2,1,0:T(4,128)S(1)}, f32[2,4,256,256]{2,3,1,0:T(8,128)}) fusion(pred[2,256]{1,0:T(4,128)(4,1)S(1)} %iota_compare_fusion, bf16[2,256,1,4,80]{1,0,4,3,2:T(2,128)(2,1)} %get-tuple-element.18, bf16[2,256,1,4,80]{1,0,4,3,2:T(2,128)(2,1)} %get-tuple-element.17), kind=kOutput, calls=%fused_computation.154 | convolution fusion | flops 85983488 | bytes 2761216 | tf_op jit(solution)/shard_map/sub | solution.py:71
  22.2 1.9 fusion.56
  24.1 0.3 copy.33
  24.4 0.5 dot_general.23
  24.9 3.5 %fusion.60 = f32[128,4,1280]{2,0,1:T(8,128)} fusion(bf16[320,1280]{1,0:T(8,128)(2,1)} %param.20, bf16[128,4,320]{2,1,0:T(4,128)(2,1)S(1)} %dot_general.23), kind=kOutput, calls=%fused_computation.82 | convolution fusion | flops 419430400 | bytes 3768320 | tf_op jit(solution)/shard_map/dot_general | solution.py:76
  28.5 0.5 all-gather.7.cloned.1.call-update
  29.1 3.5 %reshape.160 = bf16[128,4,1280]{2,1,0:T(4,128)(2,1)} reshape(bf16[512,1280]{1,0:T(8,128)(2,1)} %param.16) | data formatting | bytes 2621440 | tf_op jit(solution)/shard_map/reshape | solution.py:79
  32.6 2.0 constant_dynamic-slice_fusion
  34.6 49.0 %reduce-scatter.3.cloned.1.call-done = f32[128,1,1280]{2,0,1:T(8,128)} async-done(((f32[128,4,1280]{2,0,1:T(8,128)}), f32[128,1,1280]{2,0,1:T(8,128)}) %reduce-scatter.3.cloned.1.call-update) | async-done | bytes 655376 | tf_op jit(solution)/shard_map/reduce_scatter | solution.py:81
  83.6 1.2 convert_reduce_fusion.1
  84.8 0.2 fusion.65
  85.1 1.0 fusion.67
  86.1 0.5 all-gather.9.cloned.1.call-update
  86.7 17.1 %all-gather.5.cloned.1.call-done = bf16[512,1280]{1,0:T(8,128)(2,1)} async-done(((bf16[128,1280]{1,0:T(8,128)(2,1)}), bf16[512,1280]{1,0:T(8,128)(2,1)}) %all-gather.5.cloned.1.call-update) | async-done | bytes 1310736 | tf_op jit(solution)/shard_map/all_gather | solution.py:92
  103.8 5.8 %fusion.110 = f32[512,1280]{1,0:T(8,128)} fusion(bf16[512,1280]{1,0:T(8,128)(2,1)} %all-gather.5.cloned.1.call-done, bf16[1280,1280]{1,0:T(8,128)(2,1)} %all-gather.7.cloned.1.call-done), kind=kOutput, calls=%fused_computation.155 | convolution fusion | flops 1677721600 | bytes 7208960 | tf_op jit(solution)/shard_map/dot_general | solution.py:91
  109.6 0.6 copy-done.7
  110.2 4.5 %all-gather = bf16[2,1,640]{2,1,0:T(2,128)(2,1)S(1)} all-gather(bf16[1,1,640]{2,1,0:T(2,128)(2,1)S(1)} %reshape.198), channel_id=1, replica_groups=mesh['section'=2,'dp'=4,'mp'=4] {'section'}, dimensions={0}, use_global_device_ids=true | all-gather | bytes 3840 | tf_op jit(solution)/shard_map/all_gather | solution.py:89
  114.8 58.8 %all-gather.9.cloned.1.call-done = bf16[1280,2048]{1,0:T(8,128)(2,1)} async-done(((bf16[640,2048]{1,0:T(8,128)(2,1)}), bf16[1280,2048]{1,0:T(8,128)(2,1)}) %all-gather.9.cloned.1.call-update) | async-done | bytes 5242896 | tf_op jit(solution)/shard_map/all_gather | solution.py:88
  173.6 40.2 %all-reduce.2.cloned.1.call-done = f32[512,1280]{1,0:T(8,128)} async-done(((f32[512,1280]{1,0:T(8,128)}), f32[512,1280]{1,0:T(8,128)}) %all-reduce.2.cloned.1.call-update) | async-done | bytes 2621456 | tf_op jit(solution)/shard_map/psum | solution.py:96
  213.8 12.1 %convolution_convert_fusion = bf16[512,2048]{1,0:T(8,128)(2,1)} fusion(bf16[1280,2048]{1,0:T(8,128)(2,1)} %all-gather.9.cloned.1.call-done, f32[512,1280]{1,0:T(8,128)} %all-reduce.2.cloned.1.call-done, f32[1280]{0:T(1024)S(1)} %reshape.200), kind=kOutput, calls=%fused_computation.14 | convolution fusion | flops 2728656896 | bytes 9966592 | tf_op jit(solution)/shard_map/dot_general | solution.py:101
  225.9 4.7 %collective-permute-start = (bf16[512,2048]{1,0:T(8,128)(2,1)}, bf16[512,2048]{1,0:T(8,128)(2,1)}, u32[]{:S(2)}, u32[]{:S(2)}) collective-permute-start(bf16[512,2048]{1,0:T(8,128)(2,1)} %param.28), channel_id=1, source_target_pairs={{0,16},{1,17},{2,18},{3,19},{4,20},{5,21},{6,22},{7,23},{8,24},{9,... | collective-permute-start | bytes 6291464 | tf_op jit(solution)/shard_map/ppermute | solution.py:17
  230.7 0.6 fusion.108
  231.3 1.3 compare_select_fusion.2
  232.6 0.1 reshape.157
  232.6 0.1 reshape.178
  232.7 0.1 fusion.70
  232.8 1.2 scatter_custom_fusion
  234.0 3.3 %all-to-all-start = ((s32[8,1,16]{2,1,0:T(1,128)}), s32[8,1,16]{2,1,0:T(1,128)S(1)}, u32[]{:S(2)}, u32[]{:S(2)}) async-start(s32[8,1,16]{2,1,0:T(1,128)} %bitcast.3), calls=%async_computation | async-start | bytes 8192 | tf_op jit(solution)/shard_map/all_to_all | solution.py:125
  237.3 19.0 %reduce-scatter.5.cloned.1.call-done = bf16[128,2048]{1,0:T(8,128)(2,1)} async-done(((bf16[512,2048]{1,0:T(8,128)(2,1)}), bf16[128,2048]{1,0:T(8,128)(2,1)}) %reduce-scatter.5.cloned.1.call-update) | async-done | bytes 524304 | tf_op jit(solution)/shard_map/reduce_scatter | solution.py:100
  256.3 1.1 add_convert_fusion
  257.4 0.8 broadcast_in_dim.20
  258.3 2.4 scatter_fusion
  260.7 13.7 %all-to-all-done = s32[8,1,16]{2,1,0:T(1,128)S(1)} async-done(((s32[8,1,16]{2,1,0:T(1,128)}), s32[8,1,16]{2,1,0:T(1,128)S(1)}, u32[]{:S(2)}, u32[]{:S(2)}) %all-to-all-start) | async-done | bytes 544 | tf_op jit(solution)/shard_map/all_to_all | solution.py:125
  274.4 4.7 %all-to-all-start.1 = ((bf16[8,16,2048]{2,1,0:T(8,128)(2,1)}), bf16[8,16,2048]{2,1,0:T(8,128)(2,1)S(1)}, u32[]{:S(2)}, u32[]{:S(2)}) async-start(bf16[8,16,2048]{2,1,0:T(8,128)(2,1)} %scatter_fusion), calls=%async_computation.3 | async-start | bytes 1048576 | tf_op jit(solution)/shard_map/all_to_all | solution.py:124
  279.1 0.5 broadcast.190
  279.6 0.6 reduce.10
  280.2 0.1 reshape.159
  280.3 8.5 %all-to-all-done.1 = bf16[8,16,2048]{2,1,0:T(8,128)(2,1)S(1)} async-done(((bf16[8,16,2048]{2,1,0:T(8,128)(2,1)}), bf16[8,16,2048]{2,1,0:T(8,128)(2,1)S(1)}, u32[]{:S(2)}, u32[]{:S(2)}) %all-to-all-start.1) | async-done | bytes 524320 | tf_op jit(solution)/shard_map/all_to_all | solution.py:124
  288.8 4.6 %scatter_fusion.1 = bf16[512,2048]{1,0:T(8,128)(2,1)} fusion(bf16[512,2048]{1,0:T(8,128)(2,1)} %copy.70, s32[128]{0:T(128)S(1)} %fusion.74, bf16[128,2048]{1,0:T(8,128)(2,1)S(1)} %bitcast.61), kind=kCustom, calls=%fused_computation.2 | custom fusion | bytes 1573376 | tf_op jit(solution)/shard_map/scatter | solution.py:127
  293.4 2.3 fusion.1
  295.7 10.0 %psum.15 = f32[512]{0:T(512)S(1)} all-reduce(f32[512]{0:T(512)S(1)} %fusion.1), channel_id=1, replica_groups=mesh['section'=2,'dp'=4,'mp'=4] {'mp'}, use_global_device_ids=true, to_apply=%region_13.14 | all-reduce | flops 512 | bytes 4096 | tf_op jit(solution)/shard_map/psum | solution.py:134
  305.8 4.1 %fusion.3 = bf16[512,2048]{1,0:T(8,128)(2,1)} fusion(f32[2048]{0:T(1024)S(1)} %convert_element_type.88, f32[512]{0:T(512)S(1)} %add_rsqrt_fusion, bf16[512,2048]{1,0:T(8,128)(2,1)} %scatter_fusion.1, bf16[512,2048]{1,0:T(8,128)(2,1)} %collective-permute-done, pred[]{:T(512)S(6)} %eq.6), kind=kLoop, calls=%fused_computation.8 | loop fusion | flops 5242880 | bytes 6301697 | tf_op jit(solution)/shard_map/convert_element_type | solution.py:137
  (47 shorter events, 0.6 us)
Async XLA Ops:
  8.0 4.2 %copy-start = (bf16[1280,3,320]{0,2,1:T(8,128)(2,1)S(1)}, bf16[1280,3,320]{0,2,1:T(8,128)(2,1)}, u32[]{:S(2)}) copy-start(bf16[1280,3,320]{0,2,1:T(8,128)(2,1)} %param.19) | copy-start | bytes 7372804
  8.0 4.1 %copy-start.3 = (bf16[1280]{0:T(1024)(128)(2,1)S(1)}, bf16[1280]{0:T(1024)(128)(2,1)}, u32[]{:S(2)}) copy-start(bf16[1280]{0:T(1024)(128)(2,1)} %param.21) | copy-start | bytes 7684
  8.0 75.6 %reduce-scatter.3.cloned.1.call-start = ((), (), s32[]{:S(2)}) async-start(), calls=%async_computation.4 | async-start | bytes 3276800 | tf_op jit(solution)/shard_map/reduce_scatter | solution.py:81
  8.1 3.3 %copy-start.1 = (bf16[512,1280]{1,0:T(8,128)(2,1)S(1)}, bf16[512,1280]{1,0:T(8,128)(2,1)}, u32[]{:S(2)}) copy-start(bf16[512,1280]{1,0:T(8,128)(2,1)} %param.16) | copy-start | bytes 3932164
  14.8 4.1 %copy-start.8 = (s32[2]{0:T(128)S(1)}, s32[2]{0:T(128)}, u32[]{:S(2)}) copy-start(s32[2]{0:T(128)} %param.17) | copy-start | bytes 28
  18.9 3.4 %copy-start.2 = (bf16[2,256,1,4,80]{1,0,4,3,2:T(2,128)(2,1)S(1)}, bf16[2,256,1,4,80]{1,0,4,3,2:T(2,128)(2,1)}, u32[]{:S(2)}) copy-start(bf16[2,256,1,4,80]{1,0,4,3,2:T(2,128)(2,1)} %get-tuple-element.16) | copy-start | bytes 983044
  28.5 4.1 %copy-start.4 = (bf16[1280]{0:T(1024)(128)(2,1)S(1)}, bf16[1280]{0:T(1024)(128)(2,1)}, u32[]{:S(2)}) copy-start(bf16[1280]{0:T(1024)(128)(2,1)} %param.22) | copy-start | bytes 7684
  28.5 58.3 %all-gather.7.cloned.1.call-start = ((), (), s32[]{:S(2)}) async-start(), calls=%async_computation.6 | async-start | bytes 4915200 | tf_op jit(solution)/shard_map/all_gather | solution.py:87
  29.1 74.7 %all-gather.5.cloned.1.call-start = ((), (), s32[]{:S(2)}) async-start(), calls=%async_computation.5 | async-start | bytes 1638400 | tf_op jit(solution)/shard_map/all_gather | solution.py:92
  86.1 87.6 %all-gather.9.cloned.1.call-start = ((), (), s32[]{:S(2)}) async-start(), calls=%async_computation.8 | async-start | bytes 7864320 | tf_op jit(solution)/shard_map/all_gather | solution.py:88
  86.6 127.2 %all-reduce.2.cloned.1.call-start = ((), (), s32[]{:S(2)}) async-start(), calls=%async_computation.7 | async-start | bytes 5242880 | tf_op jit(solution)/shard_map/psum | solution.py:96
  109.5 0.7 copy-start.7
  109.6 146.7 %reduce-scatter.5.cloned.1.call-start = ((), (), s32[]{:S(2)}) async-start(), calls=%async_computation.9 | async-start | bytes 2621440 | tf_op jit(solution)/shard_map/reduce_scatter | solution.py:100
  114.8 116.5 %copy-start.9 = (s32[128]{0:T(128)S(1)}, s32[128]{0:T(128)}, u32[]{:S(2)}) copy-start(s32[128]{0:T(128)} %param.18) | copy-start | bytes 1540
  114.8 116.5 %copy-start.10 = (pred[128]{0:T(512)(128)(4,1)S(1)}, pred[128]{0:T(512)(128)(4,1)}, u32[]{:S(2)}) copy-start(pred[128]{0:T(512)(128)(4,1)} %constant.224) | copy-start | bytes 388
  114.8 122.4 %copy-start.5 = (bf16[2048]{0:T(1024)(128)(2,1)S(1)}, bf16[2048]{0:T(1024)(128)(2,1)}, u32[]{:S(2)}) copy-start(bf16[2048]{0:T(1024)(128)(2,1)} %param.26) | copy-start | bytes 12292
  225.9 53.1 %copy-start.6 = (bf16[2048]{0:T(1024)(128)(2,1)S(1)}, bf16[2048]{0:T(1024)(128)(2,1)}, u32[]{:S(2)}) copy-start(bf16[2048]{0:T(1024)(128)(2,1)} %param.29) | copy-start | bytes 12292
  225.9 67.4 %collective-permute-start = (bf16[512,2048]{1,0:T(8,128)(2,1)}, bf16[512,2048]{1,0:T(8,128)(2,1)}, u32[]{:S(2)}, u32[]{:S(2)}) collective-permute-start(bf16[512,2048]{1,0:T(8,128)(2,1)} %param.28), channel_id=1, source_target_pairs={{0,16},{1,17},{2,18},{3,19},{4,20},{5,21},{6,22},{7,23},{8,24},{9,... | collective-permute-start | bytes 6291464 | tf_op jit(solution)/shard_map/ppermute | solution.py:17
  234.0 40.4 %all-to-all-start = ((s32[8,1,16]{2,1,0:T(1,128)}), s32[8,1,16]{2,1,0:T(1,128)S(1)}, u32[]{:S(2)}, u32[]{:S(2)}) async-start(s32[8,1,16]{2,1,0:T(1,128)} %bitcast.3), calls=%async_computation | async-start | bytes 8192 | tf_op jit(solution)/shard_map/all_to_all | solution.py:125
  274.4 14.4 %all-to-all-start.1 = ((bf16[8,16,2048]{2,1,0:T(8,128)(2,1)}), bf16[8,16,2048]{2,1,0:T(8,128)(2,1)S(1)}, u32[]{:S(2)}, u32[]{:S(2)}) async-start(bf16[8,16,2048]{2,1,0:T(8,128)(2,1)} %scatter_fusion), calls=%async_computation.3 | async-start | bytes 1048576 | tf_op jit(solution)/shard_map/all_to_all | solution.py:124
Sparse Core Ops, SparseCore 0:
  28.6 54.9 reduce-scatter.2
  109.7 104.0 all-reduce.1
Sparse Core Ops, SparseCore 1:
  30.5 48.9 all-gather.6
  86.2 17.6 all-gather.4
  105.2 68.4 all-gather.8
  226.0 30.2 reduce-scatter.4
where the time goes:
time: 318 us; the launch traced here: 317 us
  waiting for transfers between devices  207 us (65%)
  matrix products  29.1 us (9%)
  local copies, waits for them, and re-layouts  24.8 us (8%)
  between operations  15.9 us (5%)
  blocking collectives  14.6 us (5%)
  starting transfers between devices  12.9 us (4%)
  other arithmetic  12.9 us (4%)
    all_gather x1, waiting for transfers between devices, per_device(): lax.all_gather(fc2_weight, 'section', axis=0, tiled=True)  58.8 us
    reduce_scatter x1, waiting for transfers between devices, per_device(): lax.psum_scatter(partial_proj.reshape(merged_rows, 4, width), 'mp', scatt...  49 us
    psum x1, waiting for transfers between devices, per_device(): first_total = lax.psum(first_partial, 'mp')  40.2 us
    reduce_scatter x1, waiting for transfers between devices, per_device(): lax.psum_scatter(jnp.dot(hidden, second_full, preferred_element_type=jnp....  19 us
    all_gather x1, waiting for transfers between devices, per_device(): lax.all_gather(merge_part, 'dp', axis=0, tiled=True)  17.1 us
    all_to_all x1, waiting for transfers between devices, per_device(): lax.all_to_all(send_place, ('section', 'dp'), split_axis=0, concat_axis=0...  13.7 us
    dot_general x1, matrix products, per_device(): jnp.dot(hidden, second_full, preferred_element_type=jnp.float32)  12.1 us
    psum x1, blocking collectives, per_device(): row_total = lax.psum(jnp.sum(entering * entering, axis=1), 'mp')  10 us
  transfers between devices with their start and end apart: 9, of which 7 were waited for; matrix products, arithmetic and copies ran while one was open for 9% of the time, Pallas kernels for 0%

commit v1 on v0

v1 whole, which is shorter than its diff:
```python
import jax
import jax.numpy as jnp
from jax import lax
from jax.sharding import PartitionSpec as P

HEAD_DIM = 80
HID = 8192
PATCHES_PER_ROW = 4
GROUP_AXES = ("section", "dp")

vit_eps = 1e-06
llm_eps = 1e-06


def from_behind(value, axis, steps):
    count = lax.axis_size(axis)
    first, last = (max(0, -steps), min(count, count - steps))
    return lax.ppermute(value, axis, [(source, source + steps) for source in range(first, last)])


def swap(value, axes, offset):
    count = lax.axis_size(axes)
    return lax.ppermute(value, axes, [(i, i ^ offset) for i in range(count)])


def layer_norm(values, gain):
    centred = values.astype(jnp.float32)
    centred = centred - jnp.mean(centred, axis=-1, keepdims=True)
    variance = jnp.mean(centred * centred, axis=-1, keepdims=True)
    return centred * lax.rsqrt(variance + vit_eps) * gain.astype(jnp.float32)


def gather_runs(block, bits, order):
    n = len(bits)
    for at in order:
        received = jnp.flip(swap(block, GROUP_AXES, bits[at]), n - 1 - at)
        block = jnp.concatenate([block, received], axis=n)
    return block


def scatter_runs(part, bits, order):
    n = len(bits)
    left = list(range(n))
    for at in order:
        axis = left.index(at)
        axis = len(left) - 1 - axis
        keep = lax.index_in_dim(part, 0, axis, keepdims=False)
        send = lax.index_in_dim(part, 1, axis, keepdims=False)
        received = swap(send.astype(jnp.bfloat16), GROUP_AXES, bits[at]).astype(jnp.float32)
        left.remove(at)
        received = jnp.flip(received, len(left) + 1 + (n - 1 - at))
        part = keep + received
    return part


def per_device(
    patches,
    patch_counts,
    dest_rows,
    qkv_weight,
    out_weight,
    attn_gain,
    merge_gain,
    fc1_weight,
    fc1_bias,
    fc2_weight,
    fc2_bias,
    text_embeds,
    section_hidden,
    llm_gain,
):
    width = patches.shape[1]
    tile_total = patch_counts.shape[0]
    block_rows = patches.shape[0] // tile_total
    merged_rows = patches.shape[0] // PATCHES_PER_ROW
    local_cols = qkv_weight.shape[2]
    local_heads = local_cols // HEAD_DIM
    feature_cols = text_embeds.shape[1]
    seq_rows = text_embeds.shape[0]
    group_count = lax.axis_size(GROUP_AXES)
    planes = lax.axis_size("mp")
    run_len = merged_rows // group_count
    group = lax.axis_index(GROUP_AXES)
    plane = lax.axis_index("mp")
    all_bits = [1 << i for i in range(group_count.bit_length() - 1)]
    pair_bit, bits = all_bits[0], all_bits[1:]
    n = len(bits)
    forward, backward = list(range(n)), list(range(n))[::-1]
    two = (2,) * n

    fc1_pair = jnp.concatenate([fc1_weight, swap(fc1_weight, GROUP_AXES, pair_bit)], axis=1)
    fc2_pair = jnp.concatenate([fc2_weight, swap(fc2_weight, GROUP_AXES, pair_bit)], axis=0)
    bias_pair = jnp.concatenate([fc1_bias, swap(fc1_bias, GROUP_AXES, pair_bit)], axis=0)

    share_bits = all_bits[:3]
    shares = 1 << len(share_bits)
    share = group % shares
    share_rows = local_cols // shares
    own_share = lax.dynamic_slice_in_dim(out_weight, share * share_rows, share_rows, 0)
    far = jnp.stack([swap(own_share, "mp", k) for k in range(1, planes)])
    halves = []
    for part, order in ((far[:, :, : width // 2], (1, 2, 0)), (far[:, :, width // 2 :], (2, 1, 0))):
        got = part[:, None, None, None]
        for at in order:
            bit = (share >> at) & 1
            received = swap(got, GROUP_AXES, share_bits[at])
            got = jnp.concatenate(
                [jnp.where(bit == 1, received, got), jnp.where(bit == 1, got, received)], axis=3 - at
            )
        halves.append(got.reshape((planes - 1) * local_cols, width // 2))
    out_full = jnp.concatenate([out_weight, jnp.concatenate(halves, axis=1)], axis=0)

    slot_in_tile = jnp.arange(merged_rows, dtype=jnp.int32) % (block_rows // PATCHES_PER_ROW)
    tile_counts = jnp.repeat(
        patch_counts, block_rows // PATCHES_PER_ROW, total_repeat_length=merged_rows
    )
    live = slot_in_tile * PATCHES_PER_ROW < tile_counts
    run_target = (dest_rows // seq_rows).reshape(group_count, run_len)[:, 0]
    place = jnp.where(live, dest_rows % seq_rows, seq_rows).reshape(group_count, run_len)
    offsets = jnp.arange(group_count, dtype=jnp.int32)
    is_run = (run_target[None, :] ^ group) == offsets[:, None]
    run_of = jnp.sum(jnp.where(is_run, offsets[None, :], 0), axis=1)

    def by_receiver(rows):
        rows = rows.reshape(group_count, run_len, -1)[run_of]
        return rows.reshape(two + (2, run_len, rows.shape[-1]))

    def of_receiver(rows):
        rows = by_receiver(rows)
        mine = rows[..., 0:1, :, :]
        theirs = swap(rows[..., 1:2, :, :], GROUP_AXES, pair_bit)
        return gather_runs(mine, bits, forward), gather_runs(theirs, bits, backward)

    def in_one_order(first, second):
        first = first.reshape(two + two + first.shape[n + 1 :])
        second = second.reshape(two + two + second.shape[n + 1 :])
        second = jnp.transpose(
            second, tuple(range(n)) + tuple(range(2 * n - 1, n - 1, -1)) + (2 * n, 2 * n + 1)
        )
        return jnp.stack([first, second], axis=n)

    place_rows = in_one_order(*of_receiver(place.reshape(merged_rows, 1)))
    place_rows = place_rows[(0,) * n].reshape(-1)

    normed_in = layer_norm(patches, attn_gain).astype(jnp.bfloat16)
    projections = jnp.dot(
        normed_in, qkv_weight.reshape(width, 3 * local_cols), preferred_element_type=jnp.float32
    ).astype(jnp.bfloat16)
    projections = projections.reshape(tile_total, block_rows, 3, local_heads, HEAD_DIM)
    query_part = projections[:, :, 0]
    key_part = projections[:, :, 1]
    value_part = projections[:, :, 2]
    scores = jnp.einsum(
        "tqhd,tkhd->thqk", query_part, key_part, preferred_element_type=jnp.float32
    ) * HEAD_DIM ** (-0.5)
    key_live = (
        jnp.arange(block_rows, dtype=jnp.int32)[None, None, None, :]
        < patch_counts[:, None, None, None]
    )
    scores = jnp.where(key_live, scores, -1e30)
    weights = jax.nn.softmax(scores, axis=-1).astype(jnp.bfloat16)
    attended = jnp.einsum(
        "thqk,tkhd->tqhd", weights, value_part, preferred_element_type=jnp.float32
    ).astype(jnp.bfloat16)
    attended = attended.reshape(merged_rows, PATCHES_PER_ROW, local_cols)

    def patch_of(values, index):
        return lax.dynamic_slice_in_dim(values, index, 1, 1).reshape(merged_rows, -1)

    heads = [patch_of(attended, plane)] + [
        swap(patch_of(attended, plane ^ k), "mp", k) for k in range(1, planes)
    ]
    proj = jnp.dot(
        jnp.concatenate(heads, axis=1), out_full, preferred_element_type=jnp.float32
    )
    own_patch = patch_of(patches.reshape(merged_rows, PATCHES_PER_ROW, width), plane)
    block_out = (own_patch.astype(jnp.float32) + proj).astype(jnp.bfloat16)
    merge_part = layer_norm(block_out, merge_gain).astype(jnp.bfloat16)

    merge_rows = in_one_order(*of_receiver(merge_part))
    merge_rows = merge_rows.reshape(-1, width)
    row_count = merge_rows.shape[0]
    first_partial = jnp.dot(merge_rows, fc1_pair, preferred_element_type=jnp.float32)
    first_partial = first_partial.reshape(planes, row_count // planes, -1)

    def chunk_of(index):
        return lax.dynamic_index_in_dim(first_partial, index, 0, keepdims=False)

    first_total = chunk_of(plane)
    for k in range(1, planes):
        first_total = first_total + swap(
            chunk_of(plane ^ k).astype(jnp.bfloat16), "mp", k
        ).astype(jnp.float32)
    hidden = jax.nn.gelu(first_total + bias_pair.astype(jnp.float32), approximate=False).astype(
        jnp.bfloat16
    )
    hidden_full = lax.all_to_all(
        jnp.broadcast_to(hidden[None], (planes,) + hidden.shape), "mp", 0, 0, tiled=True
    ).reshape(row_count, -1)

    section_hidden, _ = lax.optimization_barrier((section_hidden, merge_rows))
    incoming = from_behind(section_hidden, "section", 1)

    sides = []
    half = feature_cols // 2
    for at, order in enumerate((forward, backward)):
        side = jnp.dot(
            hidden_full,
            fc2_pair[:, at * half : (at + 1) * half],
            preferred_element_type=jnp.float32,
        )
        side = side.reshape(two + (2,) + two + (run_len, half))
        side = scatter_runs(side, bits, order).reshape(-1, half)
        side_bias = fc2_bias[at * half : (at + 1) * half].astype(jnp.float32)
        sides.append((side + side_bias).astype(jnp.bfloat16))
    embeds = jnp.concatenate(sides, axis=-1)

    hit = place_rows[None, :] == jnp.arange(seq_rows, dtype=jnp.int32)[:, None]
    placed = jnp.dot(hit.astype(jnp.bfloat16), embeds, preferred_element_type=jnp.float32)
    sequence_embeds = jnp.where(
        jnp.any(hit, axis=1, keepdims=True), placed.astype(jnp.bfloat16), text_embeds
    )
    entering = jnp.where(lax.axis_index("section") == 0, sequence_embeds, incoming).astype(
        jnp.float32
    )
    own_total = jnp.sum(entering * entering, axis=1)
    row_total = own_total
    for k in range(1, planes):
        row_total = row_total + swap(own_total, "mp", k)
    layer_inputs = (
        entering * lax.rsqrt(row_total / HID + llm_eps)[:, None] * llm_gain.astype(jnp.float32)
    ).astype(jnp.bfloat16)
    return (sequence_embeds, layer_inputs)


def solution(mesh):
    in_specs = (
        P(("section", "dp"), None),
        P(("section", "dp")),
        P(("section", "dp")),
        P(None, None, "mp"),
        P("mp", None),
        P(),
        P(),
        P("mp", ("section", "dp")),
        P(("section", "dp")),
        P(("section", "dp"), "mp"),
        P("mp"),
        P(("section", "dp"), "mp"),
        P(("section", "dp"), "mp"),
        P("mp"),
    )
    out_specs = (P(("section", "dp"), "mp"), P(("section", "dp"), "mp"))
    return jax.shard_map(
        per_device, mesh=mesh, in_specs=in_specs, out_specs=out_specs, check_vma=False
    )
```

time: 318 us -> 215 us (0.68)
  waiting for transfers between devices: 207 us -> 105 us
  starting transfers between devices: 12.9 us -> 52.9 us
  blocking collectives: 14.6 us -> 0 us
  between operations: 15.9 us -> 1.54 us
  matrix products: 29.1 us -> 18.2 us
    ppermute x0 -> x35, waiting for transfers between devices: none -> 105 us  [swap(): return lax.ppermute(value, axes, [(i, i ^ offset) for i in range(count)])]
    all_gather x3 -> x0, waiting for transfers between devices: 75.9 us -> none  [the longest x1 58.8 us: per_device(): lax.all_gather(fc2_weight, 'section', axis=0, tiled=True)]
    reduce_scatter x2 -> x0, waiting for transfers between devices: 68 us -> none  [the longest x1 49 us: per_device(): lax.psum_scatter(partial_proj.reshape(merged_rows, 4, width), 'mp', scatt...]
    ppermute x0 -> x35, starting transfers between devices: none -> 42.7 us  [swap(): return lax.ppermute(value, axes, [(i, i ^ offset) for i in range(count)])]
    psum x1 -> x0, waiting for transfers between devices: 40.2 us -> none  [per_device(): first_total = lax.psum(first_partial, 'mp')]
    all_to_all x2 -> x1, waiting for transfers between devices: 22.1 us -> 0.01 us  [per_device(): lax.all_to_all(jnp.broadcast_to(hidden[None], (planes,) + hidden.shape),...]
    psum x1 -> x0, blocking collectives: 10 us -> none  [per_device(): row_total = lax.psum(jnp.sum(entering * entering, axis=1), 'mp')]
    dot_general x3 -> x5, matrix products: 21.4 us -> 12.4 us  [the longest x2 6.65 us: per_device(): jnp.dot(hidden_full, fc2_pair[:, at * half:(at + 1) * half], preferred_el...]
  transfers between devices with their start and end apart: 9 -> 37, of which waited for: 7 -> 19; matrix products, arithmetic and copies ran while one was open for 9% -> 19% of each run, Pallas kernels for 0% -> 0%
where the time goes in v1:
time: 215 us; the launch traced here: 212 us
  waiting for transfers between devices  105 us (49%)
  starting transfers between devices  52.9 us (25%)
  local copies, waits for them, and re-layouts  22.4 us (10%)
  matrix products  18.2 us (8%)
  other arithmetic  12.6 us (6%)
    ppermute x35, waiting for transfers between devices, swap(): return lax.ppermute(value, axes, [(i, i ^ offset) for i in range(count)])  105 us
    ppermute x35, starting transfers between devices, swap(): return lax.ppermute(value, axes, [(i, i ^ offset) for i in range(count)])  42.7 us
    dot_general x2, matrix products, per_device(): jnp.dot(hidden_full, fc2_pair[:, at * half:(at + 1) * half], preferred_el...  6.65 us
    unnamed x47, local copies, waits for them, and re-layouts  6.46 us
    all_to_all x1, starting transfers between devices, per_device(): lax.all_to_all(jnp.broadcast_to(hidden[None], (planes,) + hidden.shape),...  6.41 us
  transfers between devices with their start and end apart: 37, of which 19 were waited for; matrix products, arithmetic and copies ran while one was open for 19% of the time, Pallas kernels for 0%

profile of v1, /device:TPU:0, one launch (start us, length us, event | category | flops | bytes accessed | tf_op | source)
XLA Modules:
  0.0 212.4 jit_solution(11765130035615786251)
XLA Ops:
  0.7 1.7 constant_dynamic-slice_fusion
  2.4 3.1 %collective-permute-start.8 = (bf16[40,1280]{1,0:T(8,128)(2,1)}, bf16[40,1280]{1,0:T(8,128)(2,1)S(1)}, u32[]{:S(2)}, u32[]{:S(2)}) collective-permute-start(bf16[40,1280]{1,0:T(8,128)(2,1)} %constant_dynamic-slice_fusion), channel_id=1, source_target_pairs={{0,1},{1,0},{2,3},{3,2},{4,5},{5,4},{6,7},{7,6},{8,9},{9,8},{10,11... | collective-permute-start | bytes 307208 | tf_op jit(solution)/shard_map/ppermute | solution.py:23
  5.4 2.6 %collective-permute-start.9 = (bf16[40,1280]{1,0:T(8,128)(2,1)}, bf16[40,1280]{1,0:T(8,128)(2,1)}, u32[]{:S(2)}, u32[]{:S(2)}) collective-permute-start(bf16[40,1280]{1,0:T(8,128)(2,1)} %constant_dynamic-slice_fusion), channel_id=1, source_target_pairs={{0,2},{1,3},{2,0},{3,1},{4,6},{5,7},{6,4},{7,5},{8,10},{9,11},{10,... | collective-permute-start | bytes 307208 | tf_op jit(solution)/shard_map/ppermute | solution.py:23
  8.0 1.7 convert_reduce_fusion
  10.3 1.6 convolution_convert_fusion.1
  13.1 2.2 %fusion.88 = (f32[2,4,256]{2,1,0:T(4,128)S(1)}, f32[2,4,256,256]{2,3,1,0:T(8,128)}) fusion(pred[2,256]{1,0:T(4,128)(4,1)S(1)} %iota_compare_fusion.3, bf16[2,256,1,4,80]{1,0,4,3,2:T(2,128)(2,1)S(1)} %get-tuple-element.23, bf16[2,256,1,4,80]{1,0,4,3,2:T(2,128)(2,1)S(1)} %get-tuple-element.22), kind=kOutput, calls=%fused_computation.188 | convolution fusion | flops 85983488 | bytes 2761216 | tf_op jit(solution)/shard_map/sub | solution.py:161
  15.2 1.9 fusion.36
  20.1 3.5 %collective-permute-start.6 = (bf16[128,320]{0,1:T(8,128)(2,1)S(1)}, bf16[128,320]{0,1:T(8,128)(2,1)S(1)}, u32[]{:S(2)}, u32[]{:S(2)}) collective-permute-start(bf16[128,320]{0,1:T(8,128)(2,1)S(1)} %bitcast.158), channel_id=1, source_target_pairs={{0,2},{1,3},{2,0},{3,1},{4,6},{5,7},{6,4},{7,5},{8,10},{9,11},{10,... | collective-permute-start | bytes 245768 | tf_op jit(solution)/shard_map/ppermute | solution.py:23
  24.5 1.3 and_select_fusion
  27.2 1.8 collective-permute-start.14
  30.4 1.6 collective-permute-start.11
  32.6 1.7 collective-permute-start.15
  34.3 3.0 %collective-permute-done.11 = bf16[3,1,1,1,40,640]{5,4,3,2,1,0:T(8,128)(2,1)S(1)} collective-permute-done((bf16[3,1,1,1,40,640]{5,4,3,2,1,0:T(8,128)(2,1)S(1)}, bf16[3,1,1,1,40,640]{5,4,3,2,1,0:T(8,128)(2,1)S(1)}, u32[]{:S(2)}, u32[]{:S(2)}) %collective-permute-start.11) | collective-permute-done | bytes 153632 | tf_op jit(solution)/shard_map/ppermute | solution.py:23
  37.8 3.1 %collective-permute-done.15 = bf16[3,2,1,1,40,640]{5,4,0,3,2,1:T(8,128)(2,1)S(1)} collective-permute-done((bf16[3,2,1,1,40,640]{5,4,0,3,2,1:T(8,128)(2,1)S(1)}, bf16[3,2,1,1,40,640]{5,4,0,3,2,1:T(8,128)(2,1)S(1)}, u32[]{:S(2)}, u32[]{:S(2)}) %collective-permute-start.15) | collective-permute-done | bytes 307232 | tf_op jit(solution)/shard_map/ppermute | solution.py:23
  41.2 3.2 %collective-permute-done.12 = bf16[3,1,2,1,40,640]{5,4,3,2,1,0:T(8,128)(2,1)S(1)} collective-permute-done((bf16[3,1,2,1,40,640]{5,4,3,2,1,0:T(8,128)(2,1)S(1)}, bf16[3,1,2,1,40,640]{5,4,3,2,1,0:T(8,128)(2,1)S(1)}, u32[]{:S(2)}, u32[]{:S(2)}) %collective-permute-start.12) | collective-permute-done | bytes 307232 | tf_op jit(solution)/shard_map/ppermute | solution.py:23
  49.1 1.6 collective-permute-start.17
  50.7 4.6 %collective-permute-done.17 = bf16[2,2,1,16,1280]{4,3,2,1,0:T(8,128)(2,1)S(1)} collective-permute-done((bf16[2,2,1,16,1280]{4,3,2,1,0:T(8,128)(2,1)S(1)}, bf16[2,2,1,16,1280]{4,3,2,1,0:T(8,128)(2,1)S(1)}, u32[]{:S(2)}, u32[]{:S(2)}) %collective-permute-start.17) | collective-permute-done | bytes 163872 | tf_op jit(solution)/shard_map/ppermute | solution.py:23
  55.8 1.7 collective-permute-start.18
  57.6 4.9 %collective-permute-done.20 = bf16[2,2,1,16,1280]{4,3,2,1,0:T(8,128)(2,1)S(1)} collective-permute-done((bf16[2,2,1,16,1280]{4,3,2,1,0:T(8,128)(2,1)S(1)}, bf16[2,2,1,16,1280]{4,3,2,1,0:T(8,128)(2,1)S(1)}, u32[]{:S(2)}, u32[]{:S(2)}) %collective-permute-start.20) | collective-permute-done | bytes 163872 | tf_op jit(solution)/shard_map/ppermute | solution.py:23
  62.6 1.6 collective-permute-start.21
  64.1 3.6 %collective-permute-done.18 = bf16[2,2,2,16,1280]{4,3,2,1,0:T(8,128)(2,1)S(1)} collective-permute-done((bf16[2,2,2,16,1280]{4,3,2,1,0:T(8,128)(2,1)S(1)}, bf16[2,2,2,16,1280]{4,3,2,1,0:T(8,128)(2,1)S(1)}, u32[]{:S(2)}, u32[]{:S(2)}) %collective-permute-start.18) | collective-permute-done | bytes 327712 | tf_op jit(solution)/shard_map/ppermute | solution.py:23
  67.8 1.9 collective-permute-done.21
  70.1 3.8 %fusion.10 = f32[4,128,1280]{2,1,0:T(8,128)S(1)} fusion(bf16[4,128,1280]{2,1,0:T(8,128)(2,1)S(1)} %bitcast.151, bf16[1280,640]{1,0:T(8,128)(2,1)} %collective-permute-done.22, bf16[1280,640]{1,0:T(8,128)(2,1)} %param.23), kind=kOutput, calls=%fused_computation.15 | convolution fusion | flops 1684275200 | bytes 7208960 | tf_op jit(solution)/shard_map/dot_general | solution.py:183
  74.5 3.8 %collective-permute-start.24 = (bf16[128,1280]{1,0:T(8,128)(2,1)S(1)}, bf16[128,1280]{1,0:T(8,128)(2,1)S(1)}, u32[]{:S(2)}, u32[]{:S(2)}) collective-permute-start(bf16[128,1280]{1,0:T(8,128)(2,1)S(1)} %get-tuple-element.16), channel_id=1, source_target_pairs={{0,2},{1,3},{2,0},{3,1},{4,6},{5,7},{6,4},{7,5},{8,10},{9,11},{10,... | collective-permute-start | bytes 983048 | tf_op jit(solution)/shard_map/ppermute | solution.py:23
  79.0 4.7 %collective-permute-done.26 = bf16[640]{0:T(1024)(128)(2,1)S(1)} collective-permute-done((bf16[640]{0:T(1024)(128)(2,1)S(1)}, bf16[640]{0:T(1024)(128)(2,1)S(1)}, u32[]{:S(2)}, u32[]{:S(2)}) %collective-permute-start.26) | collective-permute-done | bytes 1312 | tf_op jit(solution)/shard_map/ppermute | solution.py:23
  85.0 14.9 %collective-permute-done.24 = bf16[128,1280]{1,0:T(8,128)(2,1)S(1)} collective-permute-done((bf16[128,1280]{1,0:T(8,128)(2,1)S(1)}, bf16[128,1280]{1,0:T(8,128)(2,1)S(1)}, u32[]{:S(2)}, u32[]{:S(2)}) %collective-permute-start.24) | collective-permute-done | bytes 327712 | tf_op jit(solution)/shard_map/ppermute | solution.py:23
  99.9 1.6 fusion.43
  102.6 6.4 %all-to-all-start = ((bf16[4,128,1280]{2,1,0:T(8,128)(2,1)}), bf16[4,128,1280]{2,1,0:T(8,128)(2,1)S(1)}, u32[]{:S(2)}, u32[]{:S(2)}) async-start(bf16[4,128,1280]{2,1,0:T(8,128)(2,1)} %broadcast_in_dim.48), calls=%async_computation | async-start | bytes 2621440 | tf_op jit(solution)/shard_map/all_to_all | solution.py:197
  109.8 1.5 collective-permute-start
  111.3 3.8 %collective-permute-start.32 = (bf16[512,2048]{1,0:T(8,128)(2,1)}, bf16[512,2048]{1,0:T(8,128)(2,1)}, u32[]{:S(2)}, u32[]{:S(2)}) collective-permute-start(bf16[512,2048]{1,0:T(8,128)(2,1)} %param.28), channel_id=1, source_target_pairs={{0,16},{1,17},{2,18},{3,19},{4,20},{5,21},{6,22},{7,23},{8,24},{9,... | collective-permute-start | bytes 6291464 | tf_op jit(solution)/shard_map/ppermute | solution.py:18
  115.1 3.6 %constant_dynamic-update-slice_fusion.1 = bf16[1280,2048]{1,0:T(8,128)(2,1)} fusion(bf16[640,2048]{1,0:T(8,128)(2,1)} %param.25), kind=kLoop, calls=%fused_computation.151 | loop fusion | bytes 5242880
  118.8 2.1 collective-permute-start.1
  120.9 38.4 %collective-permute-done.3 = s32[2,2,1,16,1]{3,2,1,0,4:T(1,128)S(1)} collective-permute-done((s32[2,2,1,16,1]{3,2,1,0,4:T(1,128)S(1)}, s32[2,2,1,16,1]{3,2,1,0,4:T(1,128)S(1)}, u32[]{:S(2)}, u32[]{:S(2)}) %collective-permute-start.3) | collective-permute-done | bytes 288 | tf_op jit(solution)/shard_map/ppermute | solution.py:23
  159.9 3.6 %constant_dynamic-update-slice_fusion = bf16[1280,2048]{1,0:T(8,128)(2,1)} fusion(bf16[1280,2048]{1,0:T(8,128)(2,1)} %constant_dynamic-update-slice_fusion.1, bf16[640,2048]{1,0:T(8,128)(2,1)} %collective-permute-done.27), kind=kLoop, calls=%fused_computation.150 | loop fusion | bytes 5242880 | tf_op jit(solution)/shard_map/concatenate | solution.py:92
  163.5 3.8 %fusion.21 = f32[2,2,2,2,2,16,1024]{6,5,4,3,2,1,0:T(8,128)S(1)} fusion(bf16[2,2,2,2,2,16,1280]{6,5,4,3,2,1,0:T(8,128)(2,1)S(1)} %bitcast.149, bf16[1280,2048]{1,0:T(8,128)(2,1)} %constant_dynamic-update-slice_fusion), kind=kOutput, calls=%fused_computation.30 | convolution fusion | flops 1342177280 | bytes 6029312 | tf_op jit(solution)/shard_map/dot_general | solution.py:207
  167.4 1.6 collective-permute-start.28
  169.0 2.9 %fusion.19 = f32[512,1024]{1,0:T(8,128)S(1)} fusion(bf16[512,1280]{1,0:T(8,128)(2,1)} %bitcast.150, bf16[1280,2048]{1,0:T(8,128)(2,1)S(1)} %copy-done.9), kind=kOutput, calls=%fused_computation.27 | convolution fusion | flops 1342177280 | bytes 6029312 | tf_op jit(solution)/shard_map/dot_general | solution.py:207
  172.8 2.5 %collective-permute-start.30 = (bf16[2,2,2,2,16,1024]{5,4,3,2,1,0:T(8,128)(2,1)}, bf16[2,2,2,2,16,1024]{5,4,3,2,1,0:T(8,128)(2,1)}, u32[]{:S(2)}, u32[]{:S(2)}) collective-permute-start(bf16[2,2,2,2,16,1024]{5,4,3,2,1,0:T(8,128)(2,1)} %bitcast.49), channel_id=1, source_target_pairs={{0,16},{4,20},{8,24},{12,28},{16,0},{20,4},{24,8},{28,12},{1,17},{... | collective-permute-start | bytes 1572872 | tf_op jit(solution)/shard_map/ppermute | solution.py:23
  175.3 4.9 %collective-permute-done.28 = bf16[2,2,2,2,16,1024]{5,4,3,2,1,0:T(8,128)(2,1)S(1)} collective-permute-done((bf16[2,2,2,2,16,1024]{5,4,3,2,1,0:T(8,128)(2,1)S(1)}, bf16[2,2,2,2,16,1024]{5,4,3,2,1,0:T(8,128)(2,1)S(1)}, u32[]{:S(2)}, u32[]{:S(2)}) %collective-permute-start.28) | collective-permute-done | bytes 524320 | tf_op jit(solution)/shard_map/ppermute | solution.py:23
  181.3 2.5 %collective-permute-start.29 = (bf16[2,2,2,16,1024]{4,3,2,1,0:T(8,128)(2,1)}, bf16[2,2,2,16,1024]{4,3,2,1,0:T(8,128)(2,1)S(1)}, u32[]{:S(2)}, u32[]{:S(2)}) collective-permute-start(bf16[2,2,2,16,1024]{4,3,2,1,0:T(8,128)(2,1)} %fusion.73), channel_id=1, source_target_pairs={{0,16},{4,20},{8,24},{12,28},{16,0},{20,4},{24,8},{28,12},{1,17},{... | collective-permute-start | bytes 786440 | tf_op jit(solution)/shard_map/ppermute | solution.py:23
  183.8 4.5 %collective-permute-done.30 = bf16[2,2,2,2,16,1024]{5,4,3,2,1,0:T(8,128)(2,1)} collective-permute-done((bf16[2,2,2,2,16,1024]{5,4,3,2,1,0:T(8,128)(2,1)}, bf16[2,2,2,2,16,1024]{5,4,3,2,1,0:T(8,128)(2,1)}, u32[]{:S(2)}, u32[]{:S(2)}) %collective-permute-start.30) | collective-permute-done | bytes 524320 | tf_op jit(solution)/shard_map/ppermute | solution.py:23
  192.0 5.2 %collective-permute-done.31 = bf16[2,2,2,16,1024]{4,3,2,1,0:T(8,128)(2,1)S(1)} collective-permute-done((bf16[2,2,2,16,1024]{4,3,2,1,0:T(8,128)(2,1)S(1)}, bf16[2,2,2,16,1024]{4,3,2,1,0:T(8,128)(2,1)S(1)}, u32[]{:S(2)}, u32[]{:S(2)}) %collective-permute-start.31) | collective-permute-done | bytes 262176 | tf_op jit(solution)/shard_map/ppermute | solution.py:23
  197.5 1.3 copy-done.22
  200.1 2.1 collective-permute-start.33
  202.2 2.4 %collective-permute-start.34 = (f32[512]{0:T(512)S(1)}, f32[512]{0:T(512)S(1)}, u32[]{:S(2)}, u32[]{:S(2)}) collective-permute-start(f32[512]{0:T(512)S(1)} %get-tuple-element.52), channel_id=1, source_target_pairs={{0,2},{1,3},{2,0},{3,1},{4,6},{5,7},{6,4},{7,5},{8,10},{9,11},{10,... | collective-permute-start | bytes 6152 | tf_op jit(solution)/shard_map/ppermute | solution.py:23
  204.6 2.0 collective-permute-done.34
  206.6 3.3 %collective-permute-done.35 = f32[512]{0:T(512)S(1)} collective-permute-done((f32[512]{0:T(512)S(1)}, f32[512]{0:T(512)S(1)}, u32[]{:S(2)}, u32[]{:S(2)}) %collective-permute-start.35) | collective-permute-done | bytes 2080 | tf_op jit(solution)/shard_map/ppermute | solution.py:23
  209.9 2.4 %fusion.3 = bf16[512,2048]{1,0:T(8,128)(2,1)} fusion(f32[2048]{0:T(1024)S(1)} %convert_element_type.167, f32[512]{0:T(512)S(1)} %add_rsqrt_fusion, bf16[512,2048]{1,0:T(8,128)(2,1)S(1)} %get-tuple-element.53, bf16[512,2048]{1,0:T(8,128)(2,1)} %collective-permute-done.32, pred[]{:T(512)S(6)} %eq.64), kind=kLoop, calls=%fused_computation.7 | loop fusion | flops 5242880 | bytes 6301697 | tf_op jit(solution)/shard_map/convert_element_type | solution.py:232
  (178 shorter events, 27.4 us)
Async XLA Ops:
  0.6 9.6 %copy-start = (bf16[1280,3,320]{0,2,1:T(8,128)(2,1)S(1)}, bf16[1280,3,320]{0,2,1:T(8,128)(2,1)}, u32[]{:S(2)}) copy-start(bf16[1280,3,320]{0,2,1:T(8,128)(2,1)} %param.19) | copy-start | bytes 7372804
  0.6 9.6 %copy-start.14 = (bf16[1280]{0:T(1024)(128)(2,1)S(1)}, bf16[1280]{0:T(1024)(128)(2,1)}, u32[]{:S(2)}) copy-start(bf16[1280]{0:T(1024)(128)(2,1)} %param.21) | copy-start | bytes 7684
  2.4 23.7 %collective-permute-start.8 = (bf16[40,1280]{1,0:T(8,128)(2,1)}, bf16[40,1280]{1,0:T(8,128)(2,1)S(1)}, u32[]{:S(2)}, u32[]{:S(2)}) collective-permute-start(bf16[40,1280]{1,0:T(8,128)(2,1)} %constant_dynamic-slice_fusion), channel_id=1, source_target_pairs={{0,1},{1,0},{2,3},{3,2},{4,5},{5,4},{6,7},{7,6},{8,9},{9,8},{10,11... | collective-permute-start | bytes 307208 | tf_op jit(solution)/shard_map/ppermute | solution.py:23
  5.4 20.8 %collective-permute-start.9 = (bf16[40,1280]{1,0:T(8,128)(2,1)}, bf16[40,1280]{1,0:T(8,128)(2,1)}, u32[]{:S(2)}, u32[]{:S(2)}) collective-permute-start(bf16[40,1280]{1,0:T(8,128)(2,1)} %constant_dynamic-slice_fusion), channel_id=1, source_target_pairs={{0,2},{1,3},{2,0},{3,1},{4,6},{5,7},{6,4},{7,5},{8,10},{9,11},{10,... | collective-permute-start | bytes 307208 | tf_op jit(solution)/shard_map/ppermute | solution.py:23
  8.0 18.2 %collective-permute-start.10 = (bf16[40,1280]{1,0:T(8,128)(2,1)}, bf16[40,1280]{1,0:T(8,128)(2,1)}, u32[]{:S(2)}, u32[]{:S(2)}) collective-permute-start(bf16[40,1280]{1,0:T(8,128)(2,1)} %constant_dynamic-slice_fusion), channel_id=1, source_target_pairs={{0,3},{1,2},{2,1},{3,0},{4,7},{5,6},{6,5},{7,4},{8,11},{9,10},{10,... | collective-permute-start | bytes 307208 | tf_op jit(solution)/shard_map/ppermute | solution.py:23
  17.1 7.3 %copy-start.20 = (s32[128]{0:T(128)S(1)}, s32[128]{0:T(128)}, u32[]{:S(2)}) copy-start(s32[128]{0:T(128)} %param.18) | copy-start | bytes 1540
  17.2 7.3 %copy-start.21 = (pred[128]{0:T(512)(128)(4,1)S(1)}, pred[128]{0:T(512)(128)(4,1)}, u32[]{:S(2)}) copy-start(pred[128]{0:T(512)(128)(4,1)} %constant.255) | copy-start | bytes 388
  17.5 11.5 %copy-start.3 = (bf16[512,1280]{1,0:T(8,128)(2,1)S(1)}, bf16[512,1280]{1,0:T(8,128)(2,1)}, u32[]{:S(2)}) copy-start(bf16[512,1280]{1,0:T(8,128)(2,1)} %param.16) | copy-start | bytes 3932164
  19.0 27.9 %collective-permute-start.5 = (bf16[128,320]{0,1:T(8,128)(2,1)S(1)}, bf16[128,320]{0,1:T(8,128)(2,1)S(1)}, u32[]{:S(2)}, u32[]{:S(2)}) collective-permute-start(bf16[128,320]{0,1:T(8,128)(2,1)S(1)} %bitcast.157), channel_id=1, source_target_pairs={{0,1},{1,0},{2,3},{3,2},{4,5},{5,4},{6,7},{7,6},{8,9},{9,8},{10,11... | collective-permute-start | bytes 245768 | tf_op jit(solution)/shard_map/ppermute | solution.py:23
  20.1 26.7 %collective-permute-start.6 = (bf16[128,320]{0,1:T(8,128)(2,1)S(1)}, bf16[128,320]{0,1:T(8,128)(2,1)S(1)}, u32[]{:S(2)}, u32[]{:S(2)}) collective-permute-start(bf16[128,320]{0,1:T(8,128)(2,1)S(1)} %bitcast.158), channel_id=1, source_target_pairs={{0,2},{1,3},{2,0},{3,1},{4,6},{5,7},{6,4},{7,5},{8,10},{9,11},{10,... | collective-permute-start | bytes 245768 | tf_op jit(solution)/shard_map/ppermute | solution.py:23
  26.1 20.8 %collective-permute-start.7 = (bf16[128,320]{0,1:T(8,128)(2,1)S(1)}, bf16[128,320]{0,1:T(8,128)(2,1)S(1)}, u32[]{:S(2)}, u32[]{:S(2)}) collective-permute-start(bf16[128,320]{0,1:T(8,128)(2,1)S(1)} %bitcast.159), channel_id=1, source_target_pairs={{0,3},{1,2},{2,1},{3,0},{4,7},{5,6},{6,5},{7,4},{8,11},{9,10},{10,... | collective-permute-start | bytes 245768 | tf_op jit(solution)/shard_map/ppermute | solution.py:23
  27.2 5.3 %collective-permute-start.14 = (bf16[3,1,1,1,40,640]{5,4,0,3,2,1:T(8,128)(2,1)S(1)}, bf16[3,1,1,1,40,640]{5,4,0,3,2,1:T(8,128)(2,1)S(1)}, u32[]{:S(2)}, u32[]{:S(2)}) collective-permute-start(bf16[3,1,1,1,40,640]{5,4,0,3,2,1:T(8,128)(2,1)S(1)} %get-tuple-element.39), channel_id=1, source_target_pairs={{0,16},{4,20},{8,24},{12,28},{16,0},{20,4},{24,8},{28,12},{1,17},{... | collective-permute-start | bytes 460808 | tf_op jit(solution)/shard_map/ppermute | solution.py:23
  30.4 6.9 %collective-permute-start.11 = (bf16[3,1,1,1,40,640]{5,4,3,2,1,0:T(8,128)(2,1)S(1)}, bf16[3,1,1,1,40,640]{5,4,3,2,1,0:T(8,128)(2,1)S(1)}, u32[]{:S(2)}, u32[]{:S(2)}) collective-permute-start(bf16[3,1,1,1,40,640]{5,4,3,2,1,0:T(8,128)(2,1)S(1)} %get-tuple-element.38), channel_id=1, source_target_pairs={{0,8},{4,12},{8,0},{12,4},{16,24},{20,28},{24,16},{28,20},{1,9},{5... | collective-permute-start | bytes 460808 | tf_op jit(solution)/shard_map/ppermute | solution.py:23
  32.6 8.3 %collective-permute-start.15 = (bf16[3,2,1,1,40,640]{5,4,0,3,2,1:T(8,128)(2,1)S(1)}, bf16[3,2,1,1,40,640]{5,4,0,3,2,1:T(8,128)(2,1)S(1)}, u32[]{:S(2)}, u32[]{:S(2)}) collective-permute-start(bf16[3,2,1,1,40,640]{5,4,0,3,2,1:T(8,128)(2,1)S(1)} %pad_maximum_fusion.11), channel_id=1, source_target_pairs={{0,8},{4,12},{8,0},{12,4},{16,24},{20,28},{24,16},{28,20},{1,9},{5... | collective-permute-start | bytes 921608 | tf_op jit(solution)/shard_map/ppermute | solution.py:23
  37.4 6.9 %collective-permute-start.12 = (bf16[3,1,2,1,40,640]{5,4,3,2,1,0:T(8,128)(2,1)S(1)}, bf16[3,1,2,1,40,640]{5,4,3,2,1,0:T(8,128)(2,1)S(1)}, u32[]{:S(2)}, u32[]{:S(2)}) collective-permute-start(bf16[3,1,2,1,40,640]{5,4,3,2,1,0:T(8,128)(2,1)S(1)} %pad_maximum_fusion.10), channel_id=1, source_target_pairs={{0,16},{4,20},{8,24},{12,28},{16,0},{20,4},{24,8},{28,12},{1,17},{... | collective-permute-start | bytes 921608 | tf_op jit(solution)/shard_map/ppermute | solution.py:23
  41.1 4.2 %collective-permute-start.16 = (bf16[3,2,2,1,40,640]{5,4,0,3,2,1:T(8,128)(2,1)S(1)}, bf16[3,2,2,1,40,640]{5,4,0,3,2,1:T(8,128)(2,1)S(1)}, u32[]{:S(2)}, u32[]{:S(2)}) collective-permute-start(bf16[3,2,2,1,40,640]{5,4,0,3,2,1:T(8,128)(2,1)S(1)} %pad_maximum_fusion.6), channel_id=1, source_target_pairs={{0,4},{4,0},{8,12},{12,8},{16,20},{20,16},{24,28},{28,24},{1,5},{5... | collective-permute-start | bytes 1843208 | tf_op jit(solution)/shard_map/ppermute | solution.py:23
  44.5 2.1 collective-permute-start.13
  45.3 24.8 %collective-permute-start.22 = (bf16[1280,640]{1,0:T(8,128)(2,1)}, bf16[1280,640]{1,0:T(8,128)(2,1)}, u32[]{:S(2)}, u32[]{:S(2)}) collective-permute-start(bf16[1280,640]{1,0:T(8,128)(2,1)} %param.23), channel_id=1, source_target_pairs={{0,4},{4,0},{8,12},{12,8},{16,20},{20,16},{24,28},{28,24},{1,5},{5... | collective-permute-start | bytes 4915208 | tf_op jit(solution)/shard_map/ppermute | solution.py:23
  49.1 6.2 %collective-permute-start.17 = (bf16[2,2,1,16,1280]{4,3,2,1,0:T(8,128)(2,1)S(1)}, bf16[2,2,1,16,1280]{4,3,2,1,0:T(8,128)(2,1)S(1)}, u32[]{:S(2)}, u32[]{:S(2)}) collective-permute-start(bf16[2,2,1,16,1280]{4,3,2,1,0:T(8,128)(2,1)S(1)} %get-tuple-element.36), channel_id=1, source_target_pairs={{0,8},{4,12},{8,0},{12,4},{16,24},{20,28},{24,16},{28,20},{1,9},{5... | collective-permute-start | bytes 491528 | tf_op jit(solution)/shard_map/ppermute | solution.py:23
  50.7 4.7 %collective-permute-start.19 = (bf16[2,2,1,16,1280]{4,3,2,1,0:T(8,128)(2,1)S(1)}, bf16[2,2,1,16,1280]{4,3,2,1,0:T(8,128)(2,1)S(1)}, u32[]{:S(2)}, u32[]{:S(2)}) collective-permute-start(bf16[2,2,1,16,1280]{4,3,2,1,0:T(8,128)(2,1)S(1)} %get-tuple-element.37), channel_id=1, source_target_pairs={{0,4},{4,0},{8,12},{12,8},{16,20},{20,16},{24,28},{28,24},{1,5},{5... | collective-permute-start | bytes 491528 | tf_op jit(solution)/shard_map/ppermute | solution.py:23
  55.4 7.1 %collective-permute-start.20 = (bf16[2,2,1,16,1280]{4,3,2,1,0:T(8,128)(2,1)S(1)}, bf16[2,2,1,16,1280]{4,3,2,1,0:T(8,128)(2,1)S(1)}, u32[]{:S(2)}, u32[]{:S(2)}) collective-permute-start(bf16[2,2,1,16,1280]{4,3,2,1,0:T(8,128)(2,1)S(1)} %collective-permute-done.19), channel_id=1, source_target_pairs={{0,16},{4,20},{8,24},{12,28},{16,0},{20,4},{24,8},{28,12},{1,17},{... | collective-permute-start | bytes 491528 | tf_op jit(solution)/shard_map/ppermute | solution.py:23
  55.8 11.9 %collective-permute-start.18 = (bf16[2,2,2,16,1280]{4,3,2,1,0:T(8,128)(2,1)S(1)}, bf16[2,2,2,16,1280]{4,3,2,1,0:T(8,128)(2,1)S(1)}, u32[]{:S(2)}, u32[]{:S(2)}) collective-permute-start(bf16[2,2,2,16,1280]{4,3,2,1,0:T(8,128)(2,1)S(1)} %pad_maximum_fusion.7), channel_id=1, source_target_pairs={{0,16},{4,20},{8,24},{12,28},{16,0},{20,4},{24,8},{28,12},{1,17},{... | collective-permute-start | bytes 983048 | tf_op jit(solution)/shard_map/ppermute | solution.py:23
  62.6 7.1 %collective-permute-start.21 = (bf16[2,2,2,16,1280]{4,3,2,1,0:T(8,128)(2,1)S(1)}, bf16[2,2,2,16,1280]{4,3,2,1,0:T(8,128)(2,1)S(1)}, u32[]{:S(2)}, u32[]{:S(2)}) collective-permute-start(bf16[2,2,2,16,1280]{4,3,2,1,0:T(8,128)(2,1)S(1)} %pad_maximum_fusion.8), channel_id=1, source_target_pairs={{0,8},{4,12},{8,0},{12,4},{16,24},{20,28},{24,16},{28,20},{1,9},{5... | collective-permute-start | bytes 983048 | tf_op jit(solution)/shard_map/ppermute | solution.py:23
  70.1 8.4 %copy-start.19 = (bf16[640]{0:T(1024)(128)(2,1)S(1)}, bf16[640]{0:T(1024)(128)(2,1)}, u32[]{:S(2)}) copy-start(bf16[640]{0:T(1024)(128)(2,1)} %param.24) | copy-start | bytes 3844
  74.1 10.9 %collective-permute-start.23 = (bf16[128,1280]{1,0:T(8,128)(2,1)S(1)}, bf16[128,1280]{1,0:T(8,128)(2,1)S(1)}, u32[]{:S(2)}, u32[]{:S(2)}) collective-permute-start(bf16[128,1280]{1,0:T(8,128)(2,1)S(1)} %get-tuple-element.14), channel_id=1, source_target_pairs={{0,1},{1,0},{2,3},{3,2},{4,5},{5,4},{6,7},{7,6},{8,9},{9,8},{10,11... | collective-permute-start | bytes 983048 | tf_op jit(solution)/shard_map/ppermute | solution.py:23
  74.5 25.4 %collective-permute-start.24 = (bf16[128,1280]{1,0:T(8,128)(2,1)S(1)}, bf16[128,1280]{1,0:T(8,128)(2,1)S(1)}, u32[]{:S(2)}, u32[]{:S(2)}) collective-permute-start(bf16[128,1280]{1,0:T(8,128)(2,1)S(1)} %get-tuple-element.16), channel_id=1, source_target_pairs={{0,2},{1,3},{2,0},{3,1},{4,6},{5,7},{6,4},{7,5},{8,10},{9,11},{10,... | collective-permute-start | bytes 983048 | tf_op jit(solution)/shard_map/ppermute | solution.py:23
  78.3 21.6 %collective-permute-start.25 = (bf16[128,1280]{1,0:T(8,128)(2,1)S(1)}, bf16[128,1280]{1,0:T(8,128)(2,1)S(1)}, u32[]{:S(2)}, u32[]{:S(2)}) collective-permute-start(bf16[128,1280]{1,0:T(8,128)(2,1)S(1)} %get-tuple-element.15), channel_id=1, source_target_pairs={{0,3},{1,2},{2,1},{3,0},{4,7},{5,6},{6,5},{7,4},{8,11},{9,10},{10,... | collective-permute-start | bytes 983048 | tf_op jit(solution)/shard_map/ppermute | solution.py:23
  78.5 81.4 %collective-permute-start.27 = (bf16[640,2048]{1,0:T(8,128)(2,1)}, bf16[640,2048]{1,0:T(8,128)(2,1)}, u32[]{:S(2)}, u32[]{:S(2)}) collective-permute-start(bf16[640,2048]{1,0:T(8,128)(2,1)} %param.25), channel_id=1, source_target_pairs={{0,4},{4,0},{8,12},{12,8},{16,20},{20,16},{24,28},{28,24},{1,5},{5... | collective-permute-start | bytes 7864328 | tf_op jit(solution)/shard_map/ppermute | solution.py:23
  78.5 5.2 %collective-permute-start.26 = (bf16[640]{0:T(1024)(128)(2,1)S(1)}, bf16[640]{0:T(1024)(128)(2,1)S(1)}, u32[]{:S(2)}, u32[]{:S(2)}) collective-permute-start(bf16[640]{0:T(1024)(128)(2,1)S(1)} %copy-done.19), channel_id=1, source_target_pairs={{0,4},{4,0},{8,12},{12,8},{16,20},{20,16},{24,28},{28,24},{1,5},{5... | collective-permute-start | bytes 3848 | tf_op jit(solution)/shard_map/ppermute | solution.py:23
  102.6 60.9 %all-to-all-start = ((bf16[4,128,1280]{2,1,0:T(8,128)(2,1)}), bf16[4,128,1280]{2,1,0:T(8,128)(2,1)S(1)}, u32[]{:S(2)}, u32[]{:S(2)}) async-start(bf16[4,128,1280]{2,1,0:T(8,128)(2,1)} %broadcast_in_dim.48), calls=%async_computation | async-start | bytes 2621440 | tf_op jit(solution)/shard_map/all_to_all | solution.py:197
  109.7 9.0 %collective-permute-start.2 = (s32[2,2,1,16,1]{3,2,1,0,4:T(1,128)S(1)}, s32[2,2,1,16,1]{3,2,1,0,4:T(1,128)S(1)}, u32[]{:S(2)}, u32[]{:S(2)}) collective-permute-start(s32[2,2,1,16,1]{3,2,1,0,4:T(1,128)S(1)} %get-tuple-element.43), channel_id=1, source_target_pairs={{0,4},{4,0},{8,12},{12,8},{16,20},{20,16},{24,28},{28,24},{1,5},{5... | collective-permute-start | bytes 776 | tf_op jit(solution)/shard_map/ppermute | solution.py:23
  109.8 8.9 %copy-start.16 = (bf16[2048]{0:T(1024)(128)(2,1)S(1)}, bf16[2048]{0:T(1024)(128)(2,1)}, u32[]{:S(2)}) copy-start(bf16[2048]{0:T(1024)(128)(2,1)} %param.26) | copy-start | bytes 12292
  109.8 9.0 %collective-permute-start = (s32[2,2,1,16,1]{3,2,1,0,4:T(1,128)S(1)}, s32[2,2,1,16,1]{3,2,1,0,4:T(1,128)S(1)}, u32[]{:S(2)}, u32[]{:S(2)}) collective-permute-start(s32[2,2,1,16,1]{3,2,1,0,4:T(1,128)S(1)} %get-tuple-element.42), channel_id=1, source_target_pairs={{0,8},{4,12},{8,0},{12,4},{16,24},{20,28},{24,16},{28,20},{1,9},{5... | collective-permute-start | bytes 776 | tf_op jit(solution)/shard_map/ppermute | solution.py:23
  111.3 86.2 %collective-permute-start.32 = (bf16[512,2048]{1,0:T(8,128)(2,1)}, bf16[512,2048]{1,0:T(8,128)(2,1)}, u32[]{:S(2)}, u32[]{:S(2)}) collective-permute-start(bf16[512,2048]{1,0:T(8,128)(2,1)} %param.28), channel_id=1, source_target_pairs={{0,16},{1,17},{2,18},{3,19},{4,20},{5,21},{6,22},{7,23},{8,24},{9,... | collective-permute-start | bytes 6291464 | tf_op jit(solution)/shard_map/ppermute | solution.py:18
  118.7 40.6 %collective-permute-start.3 = (s32[2,2,1,16,1]{3,2,1,0,4:T(1,128)S(1)}, s32[2,2,1,16,1]{3,2,1,0,4:T(1,128)S(1)}, u32[]{:S(2)}, u32[]{:S(2)}) collective-permute-start(s32[2,2,1,16,1]{3,2,1,0,4:T(1,128)S(1)} %collective-permute-done.2), channel_id=1, source_target_pairs={{0,16},{4,20},{8,24},{12,28},{16,0},{20,4},{24,8},{28,12},{1,17},{... | collective-permute-start | bytes 776 | tf_op jit(solution)/shard_map/ppermute | solution.py:23
  118.8 41.1 %collective-permute-start.1 = (s32[2,2,2,16,1]{3,2,1,0,4:T(2,128)S(1)}, s32[2,2,2,16,1]{3,2,1,0,4:T(2,128)S(1)}, u32[]{:S(2)}, u32[]{:S(2)}) collective-permute-start(s32[2,2,2,16,1]{3,2,1,0,4:T(2,128)S(1)} %pad_add_fusion.3), channel_id=1, source_target_pairs={{0,16},{4,20},{8,24},{12,28},{16,0},{20,4},{24,8},{28,12},{1,17},{... | collective-permute-start | bytes 1544 | tf_op jit(solution)/shard_map/ppermute | solution.py:23
  159.3 16.0 %collective-permute-start.4 = (s32[2,2,2,16,1]{3,2,1,0,4:T(2,128)S(1)}, s32[2,2,2,16,1]{3,2,1,0,4:T(2,128)S(1)}, u32[]{:S(2)}, u32[]{:S(2)}) collective-permute-start(s32[2,2,2,16,1]{3,2,1,0,4:T(2,128)S(1)} %pad_add_fusion.4), channel_id=1, source_target_pairs={{0,8},{4,12},{8,0},{12,4},{16,24},{20,28},{24,16},{28,20},{1,9},{5... | collective-permute-start | bytes 1544 | tf_op jit(solution)/shard_map/ppermute | solution.py:23
  167.4 12.8 %collective-permute-start.28 = (bf16[2,2,2,2,16,1024]{5,4,3,2,1,0:T(8,128)(2,1)S(1)}, bf16[2,2,2,2,16,1024]{5,4,3,2,1,0:T(8,128)(2,1)S(1)}, u32[]{:S(2)}, u32[]{:S(2)}) collective-permute-start(bf16[2,2,2,2,16,1024]{5,4,3,2,1,0:T(8,128)(2,1)S(1)} %fusion.54), channel_id=1, source_target_pairs={{0,8},{4,12},{8,0},{12,4},{16,24},{20,28},{24,16},{28,20},{1,9},{5... | collective-permute-start | bytes 1572872 | tf_op jit(solution)/shard_map/ppermute | solution.py:23
  171.9 8.5 %copy-start.4 = (f32[512,1024]{1,0:T(8,128)}, f32[512,1024]{1,0:T(8,128)S(1)}, u32[]{:S(2)}) copy-start(f32[512,1024]{1,0:T(8,128)S(1)} %fusion.19) | copy-start | bytes 6291460
  172.8 15.6 %collective-permute-start.30 = (bf16[2,2,2,2,16,1024]{5,4,3,2,1,0:T(8,128)(2,1)}, bf16[2,2,2,2,16,1024]{5,4,3,2,1,0:T(8,128)(2,1)}, u32[]{:S(2)}, u32[]{:S(2)}) collective-permute-start(bf16[2,2,2,2,16,1024]{5,4,3,2,1,0:T(8,128)(2,1)} %bitcast.49), channel_id=1, source_target_pairs={{0,16},{4,20},{8,24},{12,28},{16,0},{20,4},{24,8},{28,12},{1,17},{... | collective-permute-start | bytes 1572872 | tf_op jit(solution)/shard_map/ppermute | solution.py:23
  180.6 9.0 %slice-start = ((f32[512,1024]{1,0:T(8,128)}), f32[256,1024]{1,0:T(8,128)S(1)}, s32[]{:S(2)}) async-start(f32[512,1024]{1,0:T(8,128)} %copy-done.4), calls=%async_computation.1 | async-start | bytes 2097152 | tf_op jit(solution)/shard_map/slice | solution.py:47
  181.3 10.6 %collective-permute-start.29 = (bf16[2,2,2,16,1024]{4,3,2,1,0:T(8,128)(2,1)}, bf16[2,2,2,16,1024]{4,3,2,1,0:T(8,128)(2,1)S(1)}, u32[]{:S(2)}, u32[]{:S(2)}) collective-permute-start(bf16[2,2,2,16,1024]{4,3,2,1,0:T(8,128)(2,1)} %fusion.73), channel_id=1, source_target_pairs={{0,16},{4,20},{8,24},{12,28},{16,0},{20,4},{24,8},{28,12},{1,17},{... | collective-permute-start | bytes 786440 | tf_op jit(solution)/shard_map/ppermute | solution.py:23
  190.7 6.6 %copy-start.6 = (f32[2,2,2,2,16,1024]{5,4,3,2,1,0:T(8,128)S(1)}, f32[2,2,2,2,16,1024]{5,4,3,2,1,0:T(8,128)}, u32[]{:S(2)}) copy-start(f32[2,2,2,2,16,1024]{5,4,3,2,1,0:T(8,128)} %copy-done.5) | copy-start | bytes 3145732
  190.7 6.4 %collective-permute-start.31 = (bf16[2,2,2,16,1024]{4,3,2,1,0:T(8,128)(2,1)S(1)}, bf16[2,2,2,16,1024]{4,3,2,1,0:T(8,128)(2,1)S(1)}, u32[]{:S(2)}, u32[]{:S(2)}) collective-permute-start(bf16[2,2,2,16,1024]{4,3,2,1,0:T(8,128)(2,1)S(1)} %fusion.74), channel_id=1, source_target_pairs={{0,8},{4,12},{8,0},{12,4},{16,24},{20,28},{24,16},{28,20},{1,9},{5... | collective-permute-start | bytes 786440 | tf_op jit(solution)/shard_map/ppermute | solution.py:23
  200.1 12.3 %copy-start.8 = (bf16[512,2048]{1,0:T(8,128)(2,1)}, bf16[512,2048]{1,0:T(8,128)(2,1)S(1)}, u32[]{:S(2)}) copy-start(bf16[512,2048]{1,0:T(8,128)(2,1)S(1)} %get-tuple-element.53) | copy-start | bytes 6291460
  200.1 4.5 %collective-permute-start.33 = (f32[512]{0:T(512)S(1)}, f32[512]{0:T(512)S(1)}, u32[]{:S(2)}, u32[]{:S(2)}) collective-permute-start(f32[512]{0:T(512)S(1)} %get-tuple-element.52), channel_id=1, source_target_pairs={{0,1},{1,0},{2,3},{3,2},{4,5},{5,4},{6,7},{7,6},{8,9},{9,8},{10,11... | collective-permute-start | bytes 6152 | tf_op jit(solution)/shard_map/ppermute | solution.py:23
  202.2 4.5 %collective-permute-start.34 = (f32[512]{0:T(512)S(1)}, f32[512]{0:T(512)S(1)}, u32[]{:S(2)}, u32[]{:S(2)}) collective-permute-start(f32[512]{0:T(512)S(1)} %get-tuple-element.52), channel_id=1, source_target_pairs={{0,2},{1,3},{2,0},{3,1},{4,6},{5,7},{6,4},{7,5},{8,10},{9,11},{10,... | collective-permute-start | bytes 6152 | tf_op jit(solution)/shard_map/ppermute | solution.py:23
  204.5 5.4 %collective-permute-start.35 = (f32[512]{0:T(512)S(1)}, f32[512]{0:T(512)S(1)}, u32[]{:S(2)}, u32[]{:S(2)}) collective-permute-start(f32[512]{0:T(512)S(1)} %get-tuple-element.52), channel_id=1, source_target_pairs={{0,3},{1,2},{2,1},{3,0},{4,7},{5,6},{6,5},{7,4},{8,11},{9,10},{10,... | collective-permute-start | bytes 6152 | tf_op jit(solution)/shard_map/ppermute | solution.py:23
  (13 other events, 43.1 us)
